TPU v7x, 32 devices: a whole 2x2x4 slice. The times are simulated.
32 devices in a mesh: dp: 8 (over z, x), tp: 4 (over y, core).
Axes of the slice: x: 2, y: 2, z: 4, core: 2. Of those that a mesh axis runs over, the one named last changes fastest.
Arguments:
- main: bfloat16 [16512, 1152], P('dp', 'tp'), may hold values from -6 to 6
- long_skip: bfloat16 [16512, 1152], P('dp', 'tp'), may hold values from -6 to 6
- cotangent: bfloat16 [16512, 1152], P('dp', 'tp'), may hold values from -6 to 6
- timesteps: int32 [64], P('dp'), may hold values from 0 to 999
- loss_codes: int32 [64], P('dp'), may hold values from 0 to 7
- code_weights: float32 [8], replicated, may hold values from 0.25 to 4
- item_counts: int32 [8], P('dp'), may hold values from 4 to 8, as said below
- w_skip_main: bfloat16 [1152, 1152], P('tp'), may hold values from -0.125 to 0.125
- w_skip_long: bfloat16 [1152, 1152], P('tp'), may hold values from -0.125 to 0.125
- b_skip: float32 [1152], P('tp'), may hold values from -3 to 3
- ln1_gain: float32 [1152], P('tp'), may hold values from 0.25 to 1.75
- ln1_bias: float32 [1152], P('tp'), may hold values from -2.4 to 2.4
- w_qkv: bfloat16 [3, 1152, 1152], P(None, None, 'tp'), may hold values from -0.1875 to 0.1875
- w_proj: bfloat16 [1152, 1152], P('tp'), may hold values from -1.5 to 1.5
- b_proj: float32 [1152], P('tp'), may hold values from -3 to 3
- ln2_gain: float32 [1152], P('tp'), may hold values from 0.25 to 1.75
- ln2_bias: float32 [1152], P('tp'), may hold values from -2.4 to 2.4
- w_up: bfloat16 [1152, 4608], P(None, 'tp'), may hold values from -0.1875 to 0.1875
- b_up: float32 [4608], P('tp'), may hold values from -3 to 3
- w_down: bfloat16 [4608, 1152], P('tp'), may hold values from -0.09375 to 0.09375
- b_down: float32 [1152], P('tp'), may hold values from -3 to 3
Outputs:
- out: bfloat16 [16512, 1152], P('dp', 'tp')
- d_main: bfloat16 [16512, 1152], P('dp', 'tp')
- d_long: bfloat16 [16512, 1152], P('dp', 'tp')
- g_w_skip_main: float32 [1152, 1152], P('tp')
- g_w_skip_long: float32 [1152, 1152], P('tp')
- g_b_skip: float32 [1152], P('tp')
- g_ln1_gain: float32 [1152], P('tp')
- g_ln1_bias: float32 [1152], P('tp')
- g_w_qkv: float32 [3, 1152, 1152], P(None, None, 'tp')
- g_w_proj: float32 [1152, 1152], P('tp')
- g_b_proj: float32 [1152], P('tp')
- g_ln2_gain: float32 [1152], P('tp')
- g_ln2_bias: float32 [1152], P('tp')
- g_w_up: float32 [1152, 4608], P(None, 'tp')
- g_b_up: float32 [4608], P('tp')
- g_w_down: float32 [4608, 1152], P('tp')
- g_b_down: float32 [1152], P('tp')
Inputs may be any that keep to these rules, and one draw needn't show every extreme that they name: `item_counts`: each batch group holds 4 to 8 items; some group is full and some holds exactly 4.
All inputs are finite; a program needn't handle non-finite values.
Results may differ from a plain program's by a relative error of at most 0.02.
Values may be sent and summed in bfloat16 or wider, within the bound.
A program may use at most 192 MiB of HBM per device.

v0:
```python
import math
import jax
import jax.numpy as jnp
from jax import lax
from jax.sharding import PartitionSpec as P

HEAD = 72
SEQ = 258
TSTEPS = 1000
EPSILON = 1e-06
ROOT_HALF = 0.7071067811865476
DENSITY_SCALE = 0.3989422804014327


def item_factors(timesteps, loss_codes, code_weights, group_items):
    steps_float = timesteps.astype(jnp.float32)
    phase = (steps_float / TSTEPS + 0.008) / 1.008 * (math.pi / 2.0)
    cosine = jnp.cos(phase)
    signal = cosine * cosine
    weight = jnp.minimum(1.0, 5.0 * (1.0 - signal) / signal)
    picks = (
        loss_codes[:, None] == jnp.arange(code_weights.shape[0], dtype=jnp.int32)[None, :]
    ).astype(jnp.float32)
    coded = jnp.sum(picks * code_weights[None, :], axis=1)
    valid = (jnp.arange(timesteps.shape[0], dtype=jnp.int32) < group_items).astype(jnp.float32)
    return (weight * coded * valid, valid)


def layer_norm(stream, gain, bias, width):
    totals, squares = lax.psum((jnp.sum(stream, 0), jnp.sum(stream * stream, 0)), "tp")
    mean = totals / width
    rstd = lax.rsqrt(squares / width - mean * mean + EPSILON)
    normed = (stream - mean[None, :]) * rstd[None, :]
    rounded = (normed * gain[:, None] + bias[:, None]).astype(jnp.bfloat16)
    return (normed, rstd, lax.all_gather(rounded, "tp", axis=0, tiled=True))


def norm_back(d_normed, normed, rstd, gain, width):
    g_gain = jnp.sum(d_normed * normed, 1)
    g_bias = jnp.sum(d_normed, 1)
    scaled = d_normed * gain[:, None]
    first, second = lax.psum((jnp.sum(scaled, 0), jnp.sum(scaled * normed, 0)), "tp")
    back = rstd[None, :] * (scaled - first[None, :] / width - normed * second[None, :] / width)
    return (back, g_gain, g_bias)


def reduce_back(term, local_width):
    return lax.psum_scatter(
        term(jnp.int32(0), lax.axis_size("tp") * local_width).astype(jnp.bfloat16),
        "tp",
        scatter_dimension=0,
        tiled=True,
    ).astype(jnp.float32)


def fold_back(shard, pairs):
    piece = lax.all_gather(shard, "tp", axis=0, tiled=True)
    new_acts = tuple(
        (
            jnp.einsum("fc,ct->ft", weight, piece, preferred_element_type=jnp.float32)
            for weight, acts in pairs
        )
    )
    new_weights = tuple(
        (
            jnp.einsum("ft,ct->fc", acts, piece, preferred_element_type=jnp.float32)
            for weight, acts in pairs
        )
    )
    return (new_acts, new_weights)


def split_heads(flat, heads_here):
    pair_count = flat.shape[1] // (2 * SEQ)
    shaped = flat.reshape(heads_here, HEAD, pair_count, 2, SEQ)
    return jnp.moveaxis(shaped, 2, 0)


def join_heads(blocks):
    moved = jnp.moveaxis(blocks, 0, 2)
    return moved.reshape(moved.shape[0] * moved.shape[1], -1)


def attend(block):
    query_rows, key_rows, value_rows = block
    scale = 1.0 / math.sqrt(HEAD)
    scores = (
        jnp.einsum("hdbi,hdbj->hbij", query_rows, key_rows, preferred_element_type=jnp.float32)
        * scale
    )
    peak = jnp.max(scores, axis=-1, keepdims=True)
    logsum = peak + jnp.log(jnp.sum(jnp.exp(scores - peak), axis=-1, keepdims=True))
    probs = jnp.exp(scores - logsum).astype(jnp.bfloat16)
    attended = jnp.einsum("hbij,hdbj->hdbi", probs, value_rows, preferred_element_type=jnp.float32)
    return (attended.astype(jnp.bfloat16), logsum[..., 0])


def attend_back(block):
    query_rows, key_rows, value_rows, logsum, d_attended = block
    scale = 1.0 / math.sqrt(HEAD)
    scores = (
        jnp.einsum("hdbi,hdbj->hbij", query_rows, key_rows, preferred_element_type=jnp.float32)
        * scale
    )
    probs = jnp.exp(scores - logsum[..., None])
    probs_low = probs.astype(jnp.bfloat16)
    d_probs = jnp.einsum(
        "hdbi,hdbj->hbij", d_attended, value_rows, preferred_element_type=jnp.float32
    )
    delta = jnp.sum(probs * d_probs, axis=-1, keepdims=True)
    d_scores = (probs * (d_probs - delta)).astype(jnp.bfloat16)
    d_query = (
        jnp.einsum("hbij,hdbj->hdbi", d_scores, key_rows, preferred_element_type=jnp.float32)
        * scale
    )
    d_key = (
        jnp.einsum("hbij,hdbi->hdbj", d_scores, query_rows, preferred_element_type=jnp.float32)
        * scale
    )
    d_value = jnp.einsum(
        "hbij,hdbi->hdbj", probs_low, d_attended, preferred_element_type=jnp.float32
    )
    return (d_query.astype(jnp.bfloat16), d_key.astype(jnp.bfloat16), d_value.astype(jnp.bfloat16))


def body(
    main,
    long_skip,
    cotangent,
    timesteps,
    loss_codes,
    code_weights,
    item_counts,
    w_skip_main,
    w_skip_long,
    b_skip,
    ln1_gain,
    ln1_bias,
    w_qkv,
    w_proj,
    b_proj,
    ln2_gain,
    ln2_bias,
    w_up,
    b_up,
    w_down,
    b_down,
):
    local_width = main.shape[1]
    width = w_skip_main.shape[1]
    heads_here = local_width // HEAD
    item_scale, valid = item_factors(timesteps, loss_codes, code_weights, item_counts[0])
    row_scale = jnp.repeat(item_scale, SEQ)
    row_valid = jnp.repeat(valid, SEQ)
    main_cols = main.T
    long_cols = long_skip.T
    stream = (
        lax.psum_scatter(
            jnp.einsum("dc,dt->ct", w_skip_main, main_cols, preferred_element_type=jnp.float32)
            + jnp.einsum("dc,dt->ct", w_skip_long, long_cols, preferred_element_type=jnp.float32),
            "tp",
            scatter_dimension=0,
            tiled=True,
        )
        + b_skip[:, None]
    )
    normed_one, rstd_one, full_one = layer_norm(stream, ln1_gain, ln1_bias, width)
    qkv = jnp.einsum("edc,dt->ect", w_qkv, full_one, preferred_element_type=jnp.float32).astype(
        jnp.bfloat16
    )
    query_blocks = split_heads(qkv[0], heads_here)
    key_blocks = split_heads(qkv[1], heads_here)
    value_blocks = split_heads(qkv[2], heads_here)
    attended_blocks, logsums = lax.map(attend, (query_blocks, key_blocks, value_blocks))
    attended = join_heads(attended_blocks)
    cols_here = w_proj
    projected = lax.psum_scatter(
        jnp.einsum("rc,rt->ct", cols_here, attended, preferred_element_type=jnp.float32).astype(
            jnp.bfloat16
        ),
        "tp",
        scatter_dimension=0,
        tiled=True,
    ).astype(jnp.float32)
    stream_two = stream + projected + b_proj[:, None]
    normed_two, rstd_two, full_two = layer_norm(stream_two, ln2_gain, ln2_bias, width)
    upward = (
        jnp.einsum("dc,dt->ct", w_up, full_two, preferred_element_type=jnp.float32) + b_up[:, None]
    )
    activated = jax.nn.gelu(upward, approximate=False).astype(jnp.bfloat16)
    cols_here = w_down
    result = (
        stream_two
        + lax.psum_scatter(
            jnp.einsum(
                "fc,ft->ct", cols_here, activated, preferred_element_type=jnp.float32
            ).astype(jnp.bfloat16),
            "tp",
            scatter_dimension=0,
            tiled=True,
        ).astype(jnp.float32)
        + b_down[:, None]
    )
    out = (result * row_valid[None, :]).T.astype(jnp.bfloat16)
    grad_low = (cotangent.T.astype(jnp.float32) * row_scale[None, :]).astype(jnp.bfloat16)
    grad_wide = grad_low.astype(jnp.float32)
    g_b_down = jnp.sum(grad_wide, 1)
    (d_activated,), (g_w_down,) = fold_back(grad_low, ((w_down, activated),))
    cumulative = 0.5 * (1.0 + lax.erf(upward * ROOT_HALF))
    density = jnp.exp(-0.5 * upward * upward) * DENSITY_SCALE
    d_upward = (d_activated * (cumulative + upward * density)).astype(jnp.bfloat16)
    g_b_up = jnp.sum(d_upward.astype(jnp.float32), 1)
    g_w_up = jnp.einsum("dt,ft->df", full_two, d_upward, preferred_element_type=jnp.float32)

    def up_term(start, count_rows):
        return jnp.einsum("cf,ft->ct", w_up, d_upward, preferred_element_type=jnp.float32)

    d_normed_two = reduce_back(up_term, local_width)
    back_two, g_ln2_gain, g_ln2_bias = norm_back(
        d_normed_two, normed_two, rstd_two, ln2_gain, width
    )
    d_stream_two = (back_two + grad_wide).astype(jnp.bfloat16)
    d_stream_wide = d_stream_two.astype(jnp.float32)
    g_b_proj = jnp.sum(d_stream_wide, 1)
    (d_attended,), (g_w_proj,) = fold_back(d_stream_two, ((w_proj, attended),))
    d_attended_blocks = split_heads(d_attended.astype(jnp.bfloat16), heads_here)
    d_queries, d_keys, d_values = lax.map(
        attend_back, (query_blocks, key_blocks, value_blocks, logsums, d_attended_blocks)
    )
    d_qkv = jnp.stack([join_heads(d_queries), join_heads(d_keys), join_heads(d_values)], axis=0)
    g_w_qkv = jnp.einsum("dt,ect->edc", full_one, d_qkv, preferred_element_type=jnp.float32)

    def qkv_term(start, count_rows):
        return jnp.einsum("ecr,ert->ct", w_qkv, d_qkv, preferred_element_type=jnp.float32)

    d_normed_one = reduce_back(qkv_term, local_width)
    back_one, g_ln1_gain, g_ln1_bias = norm_back(
        d_normed_one, normed_one, rstd_one, ln1_gain, width
    )
    d_stream = (back_one + d_stream_wide).astype(jnp.bfloat16)
    g_b_skip = jnp.sum(d_stream.astype(jnp.float32), 1)
    (d_main_cols, d_long_cols), (g_w_main, g_w_long) = fold_back(
        d_stream, ((w_skip_main, main_cols), (w_skip_long, long_cols))
    )
    (
        g_w_main,
        g_w_long,
        g_b_skip,
        g_ln1_gain,
        g_ln1_bias,
        g_w_qkv,
        g_w_proj,
        g_b_proj,
        g_ln2_gain,
        g_ln2_bias,
        g_w_up,
        g_b_up,
        g_w_down,
        g_b_down,
    ) = (
        lax.psum(g_w_main.astype(jnp.bfloat16), "dp").astype(jnp.float32),
        lax.psum(g_w_long.astype(jnp.bfloat16), "dp").astype(jnp.float32),
        lax.psum(g_b_skip.astype(jnp.bfloat16), "dp").astype(jnp.float32),
        lax.psum(g_ln1_gain.astype(jnp.bfloat16), "dp").astype(jnp.float32),
        lax.psum(g_ln1_bias.astype(jnp.bfloat16), "dp").astype(jnp.float32),
        lax.psum(g_w_qkv.astype(jnp.bfloat16), "dp").astype(jnp.float32),
        lax.psum(g_w_proj.astype(jnp.bfloat16), "dp").astype(jnp.float32),
        lax.psum(g_b_proj.astype(jnp.bfloat16), "dp").astype(jnp.float32),
        lax.psum(g_ln2_gain.astype(jnp.bfloat16), "dp").astype(jnp.float32),
        lax.psum(g_ln2_bias.astype(jnp.bfloat16), "dp").astype(jnp.float32),
        lax.psum(g_w_up.astype(jnp.bfloat16), "dp").astype(jnp.float32),
        lax.psum(g_b_up.astype(jnp.bfloat16), "dp").astype(jnp.float32),
        lax.psum(g_w_down.astype(jnp.bfloat16), "dp").astype(jnp.float32),
        lax.psum(g_b_down.astype(jnp.bfloat16), "dp").astype(jnp.float32),
    )
    d_main = d_main_cols.T.astype(jnp.bfloat16)
    d_long = d_long_cols.T.astype(jnp.bfloat16)
    return (
        out,
        d_main,
        d_long,
        g_w_main,
        g_w_long,
        g_b_skip,
        g_ln1_gain,
        g_ln1_bias,
        g_w_qkv,
        g_w_proj,
        g_b_proj,
        g_ln2_gain,
        g_ln2_bias,
        g_w_up,
        g_b_up,
        g_w_down,
        g_b_down,
    )


def solution(mesh):
    return jax.shard_map(
        body,
        mesh=mesh,
        in_specs=(
            P("dp", "tp"),
            P("dp", "tp"),
            P("dp", "tp"),
            P("dp"),
            P("dp"),
            P(),
            P("dp"),
            P("tp", None),
            P("tp", None),
            P("tp"),
            P("tp"),
            P("tp"),
            P(None, None, "tp"),
            P("tp", None),
            P("tp"),
            P("tp"),
            P("tp"),
            P(None, "tp"),
            P("tp"),
            P("tp", None),
            P("tp"),
        ),
        out_specs=(
            P("dp", "tp"),
            P("dp", "tp"),
            P("dp", "tp"),
            P("tp", None),
            P("tp", None),
            P("tp"),
            P("tp"),
            P("tp"),
            P(None, None, "tp"),
            P("tp", None),
            P("tp"),
            P("tp"),
            P("tp"),
            P(None, "tp"),
            P("tp"),
            P("tp", None),
            P("tp"),
        ),
        check_vma=False,
    )
```

profile of v0, /device:TPU:0, one launch (start us, length us, event | category | flops | bytes accessed | tf_op | source)
XLA Modules:
  0.0 1135.2 jit_solution(10548227006924629064)
XLA Ops:
  11.9 6.9 convolution_add_fusion
  18.9 84.4 %reduce-scatter.16.cloned.1.call-done = f32[288,2064]{1,0:T(8,128)} async-done(((f32[1152,2064]{1,0:T(8,128)}), f32[288,2064]{1,0:T(8,128)}) %reduce-scatter.16.cloned.1.call-update) | async-done | bytes 2377744
  109.4 10.3 all-reduce.3
  126.7 39.5 %all-gather.6.cloned.1.call-done = bf16[1152,2064]{1,0:T(8,128)(2,1)} async-done(((bf16[288,2064]{1,0:T(8,128)(2,1)}), bf16[1152,2064]{1,0:T(8,128)(2,1)}) %all-gather.6.cloned.1.call-update) | async-done | bytes 4755472 | tf_op jit(solution)/shard_map/all_gather | solution.py:35
  166.2 8.2 fusion.83
  176.4 6.6 reshape_squeeze.11
  183.0 6.6 reshape_squeeze.10
  203.0 23.4 %while.26 = (s32[]{:T(128)}, bf16[4,4,72,2,258]{4,2,3,1,0:T(8,128)(2,1)}, f32[4,4,2,258]{3,2,1,0:T(2,128)}, bf16[4,4,72,2,258]{4,2,3,1,0:T(8,128)(2,1)}, bf16[4,...) while((s32[]{:T(128)}, bf16[4,4,72,2,258]{4,2,3,1,0:T(8,128)(2,1)}, ...), condition=%wide.region_8.0_spmd, body=%wide.region_5.8_spmd.sunk | while | flops 157770096 | bytes 8231833 | solution.py:174
  242.0 8.4 copy.129
  250.5 50.0 %reduce-scatter.18.cloned.1.call-done = bf16[288,2064]{1,0:T(8,128)(2,1)} async-done(((bf16[1152,2064]{1,0:T(8,128)(2,1)}), bf16[288,2064]{1,0:T(8,128)(2,1)}) %reduce-scatter.18.cloned.1.call-update) | async-done | bytes 1188880
  307.6 10.3 all-reduce.2
  333.6 30.3 %all-gather.8.cloned.1.call-done = bf16[1152,2064]{1,0:T(8,128)(2,1)} async-done(((bf16[288,2064]{1,0:T(8,128)(2,1)}), bf16[1152,2064]{1,0:T(8,128)(2,1)}) %all-gather.8.cloned.1.call-update) | async-done | bytes 4755472 | tf_op jit(solution)/shard_map/all_gather | solution.py:35
  363.9 32.2 %fusion.68 = (bf16[1152,2064]{0,1:T(8,128)(2,1)S(1)}, f32[1152,2064]{0,1:T(8,128)}) fusion(f32[1152]{0:T(1024)S(1)} %copy-done.46, bf16[1152,2064]{1,0:T(8,128)(2,1)} %all-gather.8.cloned.1.call-done, bf16[1152,1152]{1,0:T(8,128)(2,1)S(1)} %copy-done), kind=kOutput, calls=%fused_computation.81 | convolution fusion | flops 5635215360 | bytes 21680640 | tf_op jit(solution)/shard_map/dc,dt->ct/dot_general | solution.py:188
  398.4 8.5 fusion.63
  406.9 8.4 copy.131
  415.3 16.6 %fusion.122 = (bf16[1152]{0:T(1024)(128)(2,1)}, bf16[1152,2064]{0,1:T(8,128)(2,1)S(1)}) fusion(f32[1152,2064]{0,1:T(8,128)} %get-tuple-element.220, bf16[1152,2064]{1,0:T(8,128)(2,1)} %all-gather.10.cloned.1.call-done, bf16[1152,1152]{1,0:T(8,128)(2,1)} %param.44), kind=kOutput, calls=%fused_computation.176 | convolution fusion | flops 5504439296 | bytes 21678336 | tf_op jit(solution)/shard_map/fc,ct->ft/dot_general | solution.py:60
  434.1 8.7 fusion.64
  442.8 8.4 copy.133
  451.4 13.8 %reduce-scatter.20.cloned.1.call-done = bf16[288,2064]{1,0:T(8,128)(2,1)} async-done(((bf16[1152,2064]{1,0:T(8,128)(2,1)}), bf16[288,2064]{1,0:T(8,128)(2,1)}) %reduce-scatter.20.cloned.1.call-update) | async-done | bytes 1188880
  467.8 50.5 %reduce-scatter.22.cloned.1.call-done = bf16[288,2064]{1,0:T(8,128)(2,1)} async-done(((bf16[1152,2064]{1,0:T(8,128)(2,1)}), bf16[288,2064]{1,0:T(8,128)(2,1)}) %reduce-scatter.22.cloned.1.call-update) | async-done | bytes 1188880
  526.9 10.3 all-reduce.1
  544.9 39.8 %all-gather.12.cloned.1.call-done = bf16[1152,2064]{1,0:T(8,128)(2,1)} async-done(((bf16[288,2064]{1,0:T(8,128)(2,1)}), bf16[1152,2064]{1,0:T(8,128)(2,1)}) %all-gather.12.cloned.1.call-update) | async-done | bytes 4755472 | tf_op jit(solution)/shard_map/all_gather | solution.py:57
  601.7 51.3 %while.27 = (s32[]{:T(128)}, bf16[4,4,72,2,258]{4,2,3,1,0:T(8,128)(2,1)}, bf16[4,4,72,2,258]{4,2,3,1,0:T(8,128)(2,1)}, bf16[4,4,72,2,258]{4,2,3,1,0:T(8,128)(2,1...) while((s32[]{:T(128)}, ...), condition=%wide.region_23.24_spmd, body=%wide.region_21.23_spmd.sunk | while | flops 390539744 | bytes 20462064 | solution.py:227
  678.8 7.7 fusion.65
  686.5 8.4 copy.135
  695.0 50.0 %reduce-scatter.24.cloned.1.call-done = bf16[288,2064]{1,0:T(8,128)(2,1)} async-done(((bf16[1152,2064]{1,0:T(8,128)(2,1)}), bf16[288,2064]{1,0:T(8,128)(2,1)}) %reduce-scatter.24.cloned.1.call-update) | async-done | bytes 1188880
  751.9 10.5 all-reduce
  770.1 11.5 %convolution_convert_fusion.4 = bf16[1152,1152]{1,0:T(8,128)(2,1)} fusion(bf16[1152,2064]{1,0:T(8,128)(2,1)} %all-gather.8.cloned.1.call-done, bf16[1152,2064]{0,1:T(8,128)(2,1)} %copy-done.49), kind=kOutput, calls=%fused_computation.102 | convolution fusion | flops 5479612416 | bytes 12165120 | tf_op jit(solution)/shard_map/dt,ft->df/dot_general | solution.py:213
  781.6 12.4 %convolution_convert_fusion.3 = bf16[1152,1152]{1,0:T(8,128)(2,1)} fusion(bf16[1152,2064]{0,1:T(8,128)(2,1)} %copy-done.50, bf16[1152,2064]{1,0:T(8,128)(2,1)} %all-gather.10.cloned.1.call-done), kind=kOutput, calls=%fused_computation.101 | convolution fusion | flops 5479612416 | bytes 12165120 | tf_op jit(solution)/shard_map/ft,ct->fc/dot_general | solution.py:66
  796.9 6.9 fusion.108
  823.3 39.2 %all-reduce.4 = (bf16[288]{0:T(512)(128)(2,1)S(1)}, bf16[288]{0:T(512)(128)(2,1)S(1)}, bf16[288]{0:T(512)(128)(2,1)S(1)}, bf16[288]{0:T(512)(128)(2,1)S(1)}, bf1...) all-reduce(bf16[288]{0:T(512)(128)(2,1)S(1)} %get-tuple-element.204, ...), channel_id=1, replica_groups=mesh['dp'=8,'tp'=4] {'dp'}, use_global_device_ids=true, to_apply=%region_32.33 | all-reduce | flops 3168 | bytes 12672 | tf_op jit(solution)/shard_map/psum | solution.py:263
  877.9 235.9 %all-reduce.8.cloned.1.call-done = (bf16[288,1152]{1,0:T(8,128)(2,1)}, bf16[288,1152]{1,0:T(8,128)(2,1)}, bf16[3,1152,288]{1,2,0:T(8,128)(2,1)}, bf16[288,1152]{...) async-done(((bf16[288,1152]{1,0:T(8,128)(2,1)}, bf16[288,1152]{1,0:T(8,128)(2,1)}, bf16[3,1152,288]{1,2,0:T(8,128)(2,1)}, ...) | async-done | bytes 9289744 | tf_op jit(solution)/shard_map/psum | solution.py:261
  (259 shorter events, 278.4 us)
Async XLA Ops:
  7.2 356.7 %copy-start = (bf16[1152,1152]{1,0:T(8,128)(2,1)S(1)}, bf16[1152,1152]{1,0:T(8,128)(2,1)}, u32[]{:S(2)}) copy-start(bf16[1152,1152]{1,0:T(8,128)(2,1)} %param.42) | copy-start | bytes 7962628
  7.2 96.1 %reduce-scatter.16.cloned.1.call-start = ((), (), s32[]{:S(2)}) async-start(), calls=%async_computation.10 | async-start | bytes 12533760
  18.8 88.0 %copy-start.30 = (f32[288]{0:T(512)S(1)}, f32[288]{0:T(512)}, u32[]{:S(2)}) copy-start(f32[288]{0:T(512)} %param.34) | copy-start | bytes 3460
  18.8 101.5 %copy-start.33 = (f32[288]{0:T(512)S(1)}, f32[288]{0:T(512)}, u32[]{:S(2)}) copy-start(f32[288]{0:T(512)} %param.35) | copy-start | bytes 3460
  18.9 101.5 %copy-start.36 = (f32[288]{0:T(512)S(1)}, f32[288]{0:T(512)}, u32[]{:S(2)}) copy-start(f32[288]{0:T(512)} %param.36) | copy-start | bytes 3460
  18.9 147.4 %all-gather.6.cloned.1.call-start = ((), (), s32[]{:S(2)}) async-start(), calls=%async_computation.5 | async-start | bytes 6266880 | tf_op jit(solution)/shard_map/all_gather | solution.py:35
  126.4 174.0 %reduce-scatter.18.cloned.1.call-start = ((), (), s32[]{:S(2)}) async-start(), calls=%async_computation.11 | async-start | bytes 6266880
  250.4 52.6 %copy-start.37 = (f32[288]{0:T(512)S(1)}, f32[288]{0:T(512)}, u32[]{:S(2)}) copy-start(f32[288]{0:T(512)} %param.39) | copy-start | bytes 3460
  250.4 113.5 %all-gather.8.cloned.1.call-start = ((), (), s32[]{:S(2)}) async-start(), calls=%async_computation.6 | async-start | bytes 6266880 | tf_op jit(solution)/shard_map/all_gather | solution.py:35
  303.0 14.9 %copy-start.32 = (f32[288]{0:T(512)S(1)}, f32[288]{0:T(512)}, u32[]{:S(2)}) copy-start(f32[288]{0:T(512)} %param.40) | copy-start | bytes 3460
  303.0 14.9 %copy-start.38 = (f32[288]{0:T(512)S(1)}, f32[288]{0:T(512)}, u32[]{:S(2)}) copy-start(f32[288]{0:T(512)} %param.41) | copy-start | bytes 3460
  324.0 91.3 %all-gather.10.cloned.1.call-start = ((), (), s32[]{:S(2)}) async-start(), calls=%async_computation.7 | async-start | bytes 6266880 | tf_op jit(solution)/shard_map/all_gather | solution.py:57
  328.0 35.9 %copy-start.46 = (f32[1152]{0:T(1024)S(1)}, f32[1152]{0:T(1024)}, u32[]{:S(2)}) copy-start(f32[1152]{0:T(1024)} %param.43) | copy-start | bytes 13828
  333.6 131.7 %reduce-scatter.20.cloned.1.call-start = ((), (), s32[]{:S(2)}) async-start(), calls=%async_computation.12 | async-start | bytes 6266880
  363.9 34.5 %copy-start.42 = (bf16[1152,1152]{1,0:T(8,128)(2,1)S(1)}, bf16[1152,1152]{1,0:T(8,128)(2,1)}, u32[]{:S(2)}) copy-start(bf16[1152,1152]{1,0:T(8,128)(2,1)} %param.44) | copy-start | bytes 7962628
  415.3 103.1 %reduce-scatter.22.cloned.1.call-start = ((), (), s32[]{:S(2)}) async-start(), calls=%async_computation.13 | async-start | bytes 6266880
  451.2 69.7 %copy-start.39 = (f32[288]{0:T(512)S(1)}, f32[288]{0:T(512)}, u32[]{:S(2)}) copy-start(f32[288]{0:T(512)} %param.45) | copy-start | bytes 3460
  451.2 133.4 %all-gather.12.cloned.1.call-start = ((), (), s32[]{:S(2)}) async-start(), calls=%async_computation.8 | async-start | bytes 6266880 | tf_op jit(solution)/shard_map/all_gather | solution.py:57
  520.9 16.3 %copy-start.2 = (bf16[2064,288]{1,0:T(8,128)(2,1)S(1)}, bf16[2064,288]{1,0:T(8,128)(2,1)}, u32[]{:S(2)}) copy-start(bf16[2064,288]{1,0:T(8,128)(2,1)} %copy.114) | copy-start | bytes 3566596
  542.2 42.5 %copy-start.45 = (bf16[288,1152]{1,0:T(8,128)(2,1)S(1)}, bf16[288,1152]{1,0:T(8,128)(2,1)}, u32[]{:S(2)}) copy-start(bf16[288,1152]{1,0:T(8,128)(2,1)} %param.38) | copy-start | bytes 1990660
  544.8 200.1 %reduce-scatter.24.cloned.1.call-start = ((), (), s32[]{:S(2)}) async-start(), calls=%async_computation.14 | async-start | bytes 6266880
  694.9 52.6 %copy-start.27 = (f32[2064]{0:T(1024)S(1)}, f32[2064]{0:T(1024)}, u32[]{:S(2)}) copy-start(f32[2064]{0:T(1024)} %copy-done.26) | copy-start | bytes 24772
  694.9 52.6 %copy-start.29 = (f32[2064]{0:T(1024)S(1)}, f32[2064]{0:T(1024)}, u32[]{:S(2)}) copy-start(f32[2064]{0:T(1024)} %copy-done.28) | copy-start | bytes 24772
  694.9 52.6 %copy-start.31 = (f32[288]{0:T(512)S(1)}, f32[288]{0:T(512)}, u32[]{:S(2)}) copy-start(f32[288]{0:T(512)} %param.34) | copy-start | bytes 3460
  694.9 52.6 %copy-start.34 = (f32[288]{0:T(512)S(1)}, f32[288]{0:T(512)}, u32[]{:S(2)}) copy-start(f32[288]{0:T(512)} %param.35) | copy-start | bytes 3460
  694.9 67.5 %copy-start.4 = (bf16[288,2064]{0,1:T(8,128)(2,1)S(1)}, bf16[288,2064]{0,1:T(8,128)(2,1)}, u32[]{:S(2)}) copy-start(bf16[288,2064]{0,1:T(8,128)(2,1)} %get-tuple-element.203) | copy-start | bytes 3566596
  694.9 115.0 %all-gather.14.cloned.1.call-start = ((), (), s32[]{:S(2)}) async-start(), calls=%async_computation.9 | async-start | bytes 6266880 | tf_op jit(solution)/shard_map/all_gather | solution.py:57
  770.1 343.8 %all-reduce.8.cloned.1.call-start = ((), (), s32[]{:S(2)}) async-start(), calls=%async_computation.15 | async-start | bytes 18579456 | tf_op jit(solution)/shard_map/psum | solution.py:261
  770.1 23.9 %slice-start.2 = ((s8[5013504]{0:T(1024)(128)(4,1)}), s8[4194304]{0:T(1024)(128)(4,1)S(1)}, s32[]{:S(2)}) async-start(s8[5013504]{0:T(1024)(128)(4,1)} %bitcast.211), calls=%async_computation.18 | async-start | bytes 8388608
  770.1 26.8 %slice-start = ((s8[5013504]{0:T(1024)(128)(4,1)}), s8[4194304]{0:T(1024)(128)(4,1)S(1)}, s32[]{:S(2)}) async-start(s8[5013504]{0:T(1024)(128)(4,1)} %bitcast.209), calls=%async_computation.16 | async-start | bytes 8388608
  781.6 15.3 %slice-start.1 = ((s8[5013504]{0:T(1024)(128)(4,1)}), s8[819200]{0:T(1024)(128)(4,1)S(1)}, s32[]{:S(2)}) async-start(s8[5013504]{0:T(1024)(128)(4,1)} %bitcast.209), calls=%async_computation.17 | async-start | bytes 1638400
  819.5 47.6 %copy-start.22 = (bf16[288,1152]{1,0:T(8,128)(2,1)S(1)}, bf16[288,1152]{1,0:T(8,128)(2,1)}, u32[]{:S(2)}) copy-start(bf16[288,1152]{1,0:T(8,128)(2,1)} %param.32) | copy-start | bytes 1990660
  (34 other events, 156.8 us)
Sparse Core Ops, SparseCore 0:
  19.0 84.3 reduce-scatter.15
  126.5 39.6 all-gather.5
  250.5 49.8 reduce-scatter.17
  324.2 39.6 all-gather.7
  365.9 39.0 all-gather.9
  415.4 49.8 reduce-scatter.19
  468.4 49.8 reduce-scatter.21
  545.0 39.6 all-gather.11
  695.0 49.8 reduce-scatter.23
  770.2 39.7 all-gather.13
  818.3 295.5 all-reduce.7
where the time goes:
time: 1140 us
  waiting for transfers between devices  601 us (53%)
  matrix products  221 us (19%)
  local copies, waits for them, and re-layouts  152 us (13%)
  blocking collectives  80.5 us (7%)
  other arithmetic  64.8 us (6%)
  between operations  15.4 us (1%)
    unnamed x16, waiting for transfers between devices  249 us
    psum x1, waiting for transfers between devices, body(): lax.psum(g_w_main.astype(jnp.bfloat16), 'dp').astype(jnp.float32)  236 us
    all_gather x2, waiting for transfers between devices, layer_norm(): return (normed, rstd, lax.all_gather(rounded, 'tp', axis=0, tiled=True))  69.8 us
    unnamed x123, local copies, waits for them, and re-layouts  63.8 us
    all_gather x3, waiting for transfers between devices, fold_back(): piece = lax.all_gather(shard, 'tp', axis=0, tiled=True)  46 us
    psum x1, blocking collectives, body(): lax.psum(g_b_skip.astype(jnp.bfloat16), 'dp').astype(jnp.float32)  39.2 us
    dot_general x4, matrix products, fold_back(): jnp.einsum('fc,ct->ft', weight, piece, preferred_element_type=jnp.float32)  32.7 us
    dot_general x1, matrix products, body(): jnp.einsum('dc,dt->ct', w_up, full_two, preferred_element_type=jnp.float32)  32.2 us
  transfers between devices with their start and end apart: 11, of which 10 were waited for; matrix products, arithmetic and copies ran while one was open for 13% of the time, Pallas kernels for 0%

commit v1 on v0

--- a/solution.py
+++ b/solution.py
@@ -3,6 +3,7 @@
 import jax.numpy as jnp
 from jax import lax
 from jax.sharding import PartitionSpec as P
+from jax.lax import all_gather
 
 HEAD = 72
 SEQ = 258
@@ -146,6 +147,11 @@
     w_down,
     b_down,
 ):
+
+    def _read_target(field_in):
+        e_next = jnp.sum(all_gather(field_in, "dp"), axis=0)
+        return e_next
+
     local_width = main.shape[1]
     width = w_skip_main.shape[1]
     heads_here = local_width // HEAD
@@ -260,7 +266,7 @@
     ) = (
         lax.psum(g_w_main.astype(jnp.bfloat16), "dp").astype(jnp.float32),
         lax.psum(g_w_long.astype(jnp.bfloat16), "dp").astype(jnp.float32),
-        lax.psum(g_b_skip.astype(jnp.bfloat16), "dp").astype(jnp.float32),
+        _read_target(g_b_skip.astype(jnp.bfloat16)).astype(jnp.float32),
         lax.psum(g_ln1_gain.astype(jnp.bfloat16), "dp").astype(jnp.float32),
         lax.psum(g_ln1_bias.astype(jnp.bfloat16), "dp").astype(jnp.float32),
         lax.psum(g_w_qkv.astype(jnp.bfloat16), "dp").astype(jnp.float32),

time: 1140 us -> 1140 us (level)
    unnamed x0 -> x1, blocking collectives: none -> 39.5 us
    psum x1 -> x0, blocking collectives: 39.2 us -> none  [body(): lax.psum(g_b_skip.astype(jnp.bfloat16), 'dp').astype(jnp.float32)]
    unnamed x123 -> x128, local copies, waits for them, and re-layouts: 63.8 us -> 63.8 us
where the time goes in v1:
time: 1140 us
  waiting for transfers between devices  599 us (53%)
  matrix products  219 us (19%)
  local copies, waits for them, and re-layouts  152 us (13%)
  blocking collectives  80.8 us (7%)
  other arithmetic  67.9 us (6%)
  between operations  16.1 us (1%)
    unnamed x16, waiting for transfers between devices  249 us
    psum x1, waiting for transfers between devices, body(): lax.psum(g_w_main.astype(jnp.bfloat16), 'dp').astype(jnp.float32)  234 us
    all_gather x2, waiting for transfers between devices, layer_norm(): return (normed, rstd, lax.all_gather(rounded, 'tp', axis=0, tiled=True))  69.8 us
    unnamed x128, local copies, waits for them, and re-layouts  63.8 us
    all_gather x3, waiting for transfers between devices, fold_back(): piece = lax.all_gather(shard, 'tp', axis=0, tiled=True)  46 us
    unnamed x1, blocking collectives  39.5 us
    dot_general x1, matrix products, body(): jnp.einsum('dc,dt->ct', w_up, full_two, preferred_element_type=jnp.float32)  32.2 us
    dot_general x4, matrix products, fold_back(): jnp.einsum('fc,ct->ft', weight, piece, preferred_element_type=jnp.float32)  30.4 us
  transfers between devices with their start and end apart: 11, of which 10 were waited for; matrix products, arithmetic and copies ran while one was open for 13% of the time, Pallas kernels for 0%

profile of v1, /device:TPU:0, one launch (start us, length us, event | category | flops | bytes accessed | tf_op | source)
XLA Modules:
  0.0 1135.2 jit_solution(6544796627202988883)
XLA Ops:
  11.9 6.9 convolution_add_fusion
  18.9 84.4 %reduce-scatter.16.cloned.1.call-done = f32[288,2064]{1,0:T(8,128)} async-done(((f32[1152,2064]{1,0:T(8,128)}), f32[288,2064]{1,0:T(8,128)}) %reduce-scatter.16.cloned.1.call-update) | async-done | bytes 2377744
  109.4 10.3 all-reduce.4
  126.7 39.5 %all-gather.7.cloned.1.call-done = bf16[1152,2064]{1,0:T(8,128)(2,1)} async-done(((bf16[288,2064]{1,0:T(8,128)(2,1)}), bf16[1152,2064]{1,0:T(8,128)(2,1)}) %all-gather.7.cloned.1.call-update) | async-done | bytes 4755472 | tf_op jit(solution)/shard_map/all_gather | solution.py:36
  166.2 8.2 fusion.83
  176.4 6.6 reshape_squeeze.11
  183.0 6.6 reshape_squeeze.10
  203.0 23.4 %while.26 = (s32[]{:T(128)}, bf16[4,4,72,2,258]{4,2,3,1,0:T(8,128)(2,1)}, f32[4,4,2,258]{3,2,1,0:T(2,128)}, bf16[4,4,72,2,258]{4,2,3,1,0:T(8,128)(2,1)}, bf16[4,...) while((s32[]{:T(128)}, bf16[4,4,72,2,258]{4,2,3,1,0:T(8,128)(2,1)}, ...), condition=%wide.region_8.0_spmd, body=%wide.region_5.8_spmd.sunk | while | flops 157770096 | bytes 8231833 | solution.py:180
  242.0 8.4 copy.129
  250.5 50.0 %reduce-scatter.18.cloned.1.call-done = bf16[288,2064]{1,0:T(8,128)(2,1)} async-done(((bf16[1152,2064]{1,0:T(8,128)(2,1)}), bf16[288,2064]{1,0:T(8,128)(2,1)}) %reduce-scatter.18.cloned.1.call-update) | async-done | bytes 1188880
  307.6 10.3 all-reduce.3
  333.6 30.3 %all-gather.9.cloned.1.call-done = bf16[1152,2064]{1,0:T(8,128)(2,1)} async-done(((bf16[288,2064]{1,0:T(8,128)(2,1)}), bf16[1152,2064]{1,0:T(8,128)(2,1)}) %all-gather.9.cloned.1.call-update) | async-done | bytes 4755472 | tf_op jit(solution)/shard_map/all_gather | solution.py:36
  363.9 32.2 %fusion.68 = (bf16[1152,2064]{0,1:T(8,128)(2,1)S(1)}, f32[1152,2064]{0,1:T(8,128)}) fusion(f32[1152]{0:T(1024)S(1)} %copy-done.44, bf16[1152,2064]{1,0:T(8,128)(2,1)} %all-gather.9.cloned.1.call-done, bf16[1152,1152]{1,0:T(8,128)(2,1)S(1)} %copy-done), kind=kOutput, calls=%fused_computation.81 | convolution fusion | flops 5635215360 | bytes 21680640 | tf_op jit(solution)/shard_map/dc,dt->ct/dot_general | solution.py:194
  398.4 8.5 fusion.63
  406.9 8.4 copy.131
  415.3 16.6 %fusion.122 = (bf16[1152]{0:T(1024)(128)(2,1)}, bf16[1152,2064]{0,1:T(8,128)(2,1)S(1)}) fusion(f32[1152,2064]{0,1:T(8,128)} %get-tuple-element.220, bf16[1152,2064]{1,0:T(8,128)(2,1)} %all-gather.11.cloned.1.call-done, bf16[1152,1152]{1,0:T(8,128)(2,1)} %param.44), kind=kOutput, calls=%fused_computation.176 | convolution fusion | flops 5504439296 | bytes 21678336 | tf_op jit(solution)/shard_map/fc,ct->ft/dot_general | solution.py:61
  434.1 8.7 fusion.64
  442.8 8.4 copy.133
  451.4 13.9 %reduce-scatter.20.cloned.1.call-done = bf16[288,2064]{1,0:T(8,128)(2,1)} async-done(((bf16[1152,2064]{1,0:T(8,128)(2,1)}), bf16[288,2064]{1,0:T(8,128)(2,1)}) %reduce-scatter.20.cloned.1.call-update) | async-done | bytes 1188880
  467.9 50.4 %reduce-scatter.22.cloned.1.call-done = bf16[288,2064]{1,0:T(8,128)(2,1)} async-done(((bf16[1152,2064]{1,0:T(8,128)(2,1)}), bf16[288,2064]{1,0:T(8,128)(2,1)}) %reduce-scatter.22.cloned.1.call-update) | async-done | bytes 1188880
  526.9 10.3 all-reduce.2
  544.9 39.8 %all-gather.13.cloned.1.call-done = bf16[1152,2064]{1,0:T(8,128)(2,1)} async-done(((bf16[288,2064]{1,0:T(8,128)(2,1)}), bf16[1152,2064]{1,0:T(8,128)(2,1)}) %all-gather.13.cloned.1.call-update) | async-done | bytes 4755472 | tf_op jit(solution)/shard_map/all_gather | solution.py:58
  601.7 51.4 %while.27 = (s32[]{:T(128)}, bf16[4,4,72,2,258]{4,2,3,1,0:T(8,128)(2,1)}, bf16[4,4,72,2,258]{4,2,3,1,0:T(8,128)(2,1)}, bf16[4,4,72,2,258]{4,2,3,1,0:T(8,128)(2,1...) while((s32[]{:T(128)}, ...), condition=%wide.region_23.24_spmd, body=%wide.region_21.23_spmd.sunk | while | flops 390539744 | bytes 20462064 | solution.py:233
  678.9 7.7 fusion.65
  686.5 8.4 copy.135
  695.0 50.0 %reduce-scatter.24.cloned.1.call-done = bf16[288,2064]{1,0:T(8,128)(2,1)} async-done(((bf16[1152,2064]{1,0:T(8,128)(2,1)}), bf16[288,2064]{1,0:T(8,128)(2,1)}) %reduce-scatter.24.cloned.1.call-update) | async-done | bytes 1188880
  751.9 10.5 all-reduce.1
  770.1 11.5 %convolution_convert_fusion.4 = bf16[1152,1152]{1,0:T(8,128)(2,1)} fusion(bf16[1152,2064]{1,0:T(8,128)(2,1)} %all-gather.9.cloned.1.call-done, bf16[1152,2064]{0,1:T(8,128)(2,1)} %copy-done.48), kind=kOutput, calls=%fused_computation.102 | convolution fusion | flops 5479612416 | bytes 12165120 | tf_op jit(solution)/shard_map/dt,ft->df/dot_general | solution.py:219
  781.6 12.4 %convolution_convert_fusion.3 = bf16[1152,1152]{1,0:T(8,128)(2,1)} fusion(bf16[1152,2064]{0,1:T(8,128)(2,1)} %copy-done.49, bf16[1152,2064]{1,0:T(8,128)(2,1)} %all-gather.11.cloned.1.call-done), kind=kOutput, calls=%fused_computation.101 | convolution fusion | flops 5479612416 | bytes 12165120 | tf_op jit(solution)/shard_map/ft,ct->fc/dot_general | solution.py:67
  796.9 6.9 fusion.108
  826.9 39.5 %all-reduce.5 = (bf16[2304]{0:T(1024)(128)(2,1)S(1)}, bf16[288]{0:T(512)(128)(2,1)S(1)}, bf16[288]{0:T(512)(128)(2,1)S(1)}, bf16[288]{0:T(512)(128)(2,1)S(1)}, b...) all-reduce(bf16[2304]{0:T(1024)(128)(2,1)S(1)} %dynamic-update-slic, ...), channel_id=2, replica_groups=mesh['dp'=8,'tp'=4] {'dp'}, use_global_device_ids=true, to_apply=%add | all-reduce | flops 5184 | bytes 20736
  879.7 234.1 %all-reduce.9.cloned.1.call-done = (bf16[288,1152]{1,0:T(8,128)(2,1)}, bf16[288,1152]{1,0:T(8,128)(2,1)}, bf16[3,1152,288]{1,2,0:T(8,128)(2,1)}, bf16[288,1152]{...) async-done(((bf16[288,1152]{1,0:T(8,128)(2,1)}, bf16[288,1152]{1,0:T(8,128)(2,1)}, bf16[3,1152,288]{1,2,0:T(8,128)(2,1)}, ...) | async-done | bytes 9289744 | tf_op jit(solution)/shard_map/psum | solution.py:267
  (267 shorter events, 279.3 us)
Async XLA Ops:
  7.2 356.7 %copy-start = (bf16[1152,1152]{1,0:T(8,128)(2,1)S(1)}, bf16[1152,1152]{1,0:T(8,128)(2,1)}, u32[]{:S(2)}) copy-start(bf16[1152,1152]{1,0:T(8,128)(2,1)} %param.42) | copy-start | bytes 7962628
  7.2 96.1 %reduce-scatter.16.cloned.1.call-start = ((), (), s32[]{:S(2)}) async-start(), calls=%async_computation.10 | async-start | bytes 12533760
  18.8 88.0 %copy-start.28 = (f32[288]{0:T(512)S(1)}, f32[288]{0:T(512)}, u32[]{:S(2)}) copy-start(f32[288]{0:T(512)} %param.34) | copy-start | bytes 3460
  18.8 101.5 %copy-start.31 = (f32[288]{0:T(512)S(1)}, f32[288]{0:T(512)}, u32[]{:S(2)}) copy-start(f32[288]{0:T(512)} %param.35) | copy-start | bytes 3460
  18.9 101.5 %copy-start.34 = (f32[288]{0:T(512)S(1)}, f32[288]{0:T(512)}, u32[]{:S(2)}) copy-start(f32[288]{0:T(512)} %param.36) | copy-start | bytes 3460
  18.9 147.4 %all-gather.7.cloned.1.call-start = ((), (), s32[]{:S(2)}) async-start(), calls=%async_computation.5 | async-start | bytes 6266880 | tf_op jit(solution)/shard_map/all_gather | solution.py:36
  126.4 174.0 %reduce-scatter.18.cloned.1.call-start = ((), (), s32[]{:S(2)}) async-start(), calls=%async_computation.11 | async-start | bytes 6266880
  250.4 52.6 %copy-start.35 = (f32[288]{0:T(512)S(1)}, f32[288]{0:T(512)}, u32[]{:S(2)}) copy-start(f32[288]{0:T(512)} %param.39) | copy-start | bytes 3460
  250.4 113.5 %all-gather.9.cloned.1.call-start = ((), (), s32[]{:S(2)}) async-start(), calls=%async_computation.6 | async-start | bytes 6266880 | tf_op jit(solution)/shard_map/all_gather | solution.py:36
  303.0 14.9 %copy-start.36 = (f32[288]{0:T(512)S(1)}, f32[288]{0:T(512)}, u32[]{:S(2)}) copy-start(f32[288]{0:T(512)} %param.41) | copy-start | bytes 3460
  324.1 91.3 %all-gather.11.cloned.1.call-start = ((), (), s32[]{:S(2)}) async-start(), calls=%async_computation.7 | async-start | bytes 6266880 | tf_op jit(solution)/shard_map/all_gather | solution.py:58
  328.0 35.9 %copy-start.44 = (f32[1152]{0:T(1024)S(1)}, f32[1152]{0:T(1024)}, u32[]{:S(2)}) copy-start(f32[1152]{0:T(1024)} %param.43) | copy-start | bytes 13828
  333.6 131.7 %reduce-scatter.20.cloned.1.call-start = ((), (), s32[]{:S(2)}) async-start(), calls=%async_computation.12 | async-start | bytes 6266880
  363.9 34.5 %copy-start.40 = (bf16[1152,1152]{1,0:T(8,128)(2,1)S(1)}, bf16[1152,1152]{1,0:T(8,128)(2,1)}, u32[]{:S(2)}) copy-start(bf16[1152,1152]{1,0:T(8,128)(2,1)} %param.44) | copy-start | bytes 7962628
  415.3 103.0 %reduce-scatter.22.cloned.1.call-start = ((), (), s32[]{:S(2)}) async-start(), calls=%async_computation.13 | async-start | bytes 6266880
  451.2 69.7 %copy-start.37 = (f32[288]{0:T(512)S(1)}, f32[288]{0:T(512)}, u32[]{:S(2)}) copy-start(f32[288]{0:T(512)} %param.45) | copy-start | bytes 3460
  451.2 133.4 %all-gather.13.cloned.1.call-start = ((), (), s32[]{:S(2)}) async-start(), calls=%async_computation.8 | async-start | bytes 6266880 | tf_op jit(solution)/shard_map/all_gather | solution.py:58
  520.9 16.3 %copy-start.2 = (bf16[2064,288]{1,0:T(8,128)(2,1)S(1)}, bf16[2064,288]{1,0:T(8,128)(2,1)}, u32[]{:S(2)}) copy-start(bf16[2064,288]{1,0:T(8,128)(2,1)} %copy.114) | copy-start | bytes 3566596
  542.2 42.5 %copy-start.43 = (bf16[288,1152]{1,0:T(8,128)(2,1)S(1)}, bf16[288,1152]{1,0:T(8,128)(2,1)}, u32[]{:S(2)}) copy-start(bf16[288,1152]{1,0:T(8,128)(2,1)} %param.38) | copy-start | bytes 1990660
  544.8 200.1 %reduce-scatter.24.cloned.1.call-start = ((), (), s32[]{:S(2)}) async-start(), calls=%async_computation.14 | async-start | bytes 6266880
  694.9 52.6 %copy-start.25 = (f32[2064]{0:T(1024)S(1)}, f32[2064]{0:T(1024)}, u32[]{:S(2)}) copy-start(f32[2064]{0:T(1024)} %copy-done.24) | copy-start | bytes 24772
  694.9 52.6 %copy-start.27 = (f32[2064]{0:T(1024)S(1)}, f32[2064]{0:T(1024)}, u32[]{:S(2)}) copy-start(f32[2064]{0:T(1024)} %copy-done.26) | copy-start | bytes 24772
  694.9 52.6 %copy-start.29 = (f32[288]{0:T(512)S(1)}, f32[288]{0:T(512)}, u32[]{:S(2)}) copy-start(f32[288]{0:T(512)} %param.34) | copy-start | bytes 3460
  694.9 52.6 %copy-start.32 = (f32[288]{0:T(512)S(1)}, f32[288]{0:T(512)}, u32[]{:S(2)}) copy-start(f32[288]{0:T(512)} %param.35) | copy-start | bytes 3460
  694.9 67.5 %copy-start.4 = (bf16[288,2064]{0,1:T(8,128)(2,1)S(1)}, bf16[288,2064]{0,1:T(8,128)(2,1)}, u32[]{:S(2)}) copy-start(bf16[288,2064]{0,1:T(8,128)(2,1)} %get-tuple-element.203) | copy-start | bytes 3566596
  694.9 115.0 %all-gather.15.cloned.1.call-start = ((), (), s32[]{:S(2)}) async-start(), calls=%async_computation.9 | async-start | bytes 6266880 | tf_op jit(solution)/shard_map/all_gather | solution.py:58
  770.1 343.7 %all-reduce.9.cloned.1.call-start = ((), (), s32[]{:S(2)}) async-start(), calls=%async_computation.15 | async-start | bytes 18579456 | tf_op jit(solution)/shard_map/psum | solution.py:267
  770.1 23.9 %slice-start.2 = ((s8[5013504]{0:T(1024)(128)(4,1)}), s8[4194304]{0:T(1024)(128)(4,1)S(1)}, s32[]{:S(2)}) async-start(s8[5013504]{0:T(1024)(128)(4,1)} %bitcast.212), calls=%async_computation.18 | async-start | bytes 8388608
  770.1 26.7 %slice-start = ((s8[5013504]{0:T(1024)(128)(4,1)}), s8[4194304]{0:T(1024)(128)(4,1)S(1)}, s32[]{:S(2)}) async-start(s8[5013504]{0:T(1024)(128)(4,1)} %bitcast.210), calls=%async_computation.16 | async-start | bytes 8388608
  781.6 15.3 %slice-start.1 = ((s8[5013504]{0:T(1024)(128)(4,1)}), s8[819200]{0:T(1024)(128)(4,1)S(1)}, s32[]{:S(2)}) async-start(s8[5013504]{0:T(1024)(128)(4,1)} %bitcast.210), calls=%async_computation.17 | async-start | bytes 1638400
  820.0 51.1 %copy-start.20 = (bf16[288,1152]{1,0:T(8,128)(2,1)S(1)}, bf16[288,1152]{1,0:T(8,128)(2,1)}, u32[]{:S(2)}) copy-start(bf16[288,1152]{1,0:T(8,128)(2,1)} %param.32) | copy-start | bytes 1990660
  825.3 51.5 %slice-start.4 = ((s8[5013504]{0:T(1024)(128)(4,1)}), s8[819200]{0:T(1024)(128)(4,1)S(1)}, s32[]{:S(2)}) async-start(s8[5013504]{0:T(1024)(128)(4,1)} %bitcast.214), calls=%async_computation.20 | async-start | bytes 1638400
  (35 other events, 175.9 us)
Sparse Core Ops, SparseCore 0:
  18.9 84.3 reduce-scatter.15
  126.5 39.6 all-gather.6
  250.5 49.8 reduce-scatter.17
  324.2 39.6 all-gather.8
  365.9 39.0 all-gather.10
  415.4 49.8 reduce-scatter.19
  468.4 49.8 reduce-scatter.21
  545.0 39.6 all-gather.12
  695.1 49.8 reduce-scatter.23
  770.2 39.7 all-gather.14
  818.3 295.5 all-reduce.8
